TPU v7x, 32 devices: a whole 2x2x4 slice. The times are simulated.
32 devices in a mesh: groups: 2 (over y), head: 4 (over z), state: 4 (over x, core).
Axes of the slice: x: 2, y: 2, z: 4, core: 2. Of those that a mesh axis runs over, the one named last changes fastest.
Arguments:
- tokens: bfloat16 [32, 2048], P(('groups', 'head'), 'state'), parts along dimension 0, may hold values from -20 to 20
- mixer_norm: float32 [2048], P('state'), may hold values from 0.1 to 1.9
- input_proj: bfloat16 [2, 2048, 8192], P(None, 'state', 'head'), may hold values from -0.125 to 0.125
- conv_weight: float32 [4, 8192], P(None, 'head'), may hold values from -3 to 3
- conv_bias: float32 [8192], P('head'), may hold values from -3 to 3
- conv_state: float32 [3, 32, 8192], P(None, 'groups', 'head'), parts along dimension 1, may hold values from -6 to 6
- state_proj: bfloat16 [8192, 288], P('head'), may hold values from -0.125 to 0.125
- step_gain: float32 [256], replicated, may hold values from 0.1 to 1.9
- step_proj: bfloat16 [256, 8192], P(None, 'head'), may hold values from -0.375 to 0.375
- step_bias: float32 [8192], P('head'), may hold values from -6 to -1
- decay_log: float32 [16, 8192], P('state', 'head'), may hold values from 0 to 2.77
- skip_gain: float32 [8192], P('head'), may hold values from 0.5 to 1.5
- ssm_state: float32 [16, 32, 8192], P('state', 'groups', 'head'), parts along dimension 1, may hold values from -6 to 6
- output_proj: bfloat16 [8192, 2048], P('head', 'state'), may hold values from -0.0625 to 0.0625
- moe_norm: float32 [2048], replicated, may hold values from 0.1 to 1.9
- router_weight: float32 [2048, 8], replicated, may hold values from -0.125 to 0.125
- expert_ids: int32 [32, 2], P(('groups', 'head')), parts along dimension 0, may hold values from 0 to 7, as said below
- slot_ids: int32 [32, 2], P(('groups', 'head')), parts along dimension 0, may hold values from 0 to 3, as said below
- gate_proj: bfloat16 [8, 2048, 7168], P('head', None, 'state'), may hold values from -0.125 to 0.125
- up_proj: bfloat16 [8, 2048, 7168], P('head', None, 'state'), may hold values from -0.125 to 0.125
- down_proj: bfloat16 [8, 7168, 2048], P('head', 'state'), may hold values from -0.0625 to 0.0625
Outputs:
- layer_out: bfloat16 [32, 2048], P(('groups', 'head'), 'state'), parts along dimension 0
- new_conv: float32 [3, 32, 8192], P(None, 'groups', 'head'), parts along dimension 1
- new_state: float32 [16, 32, 8192], P('state', 'groups', 'head'), parts along dimension 1
- expert_load: float32 [16], P('groups'), parts along dimension 0
- aux_loss: float32 [2], P('groups'), parts along dimension 0
There are 2 independent parts, one for each index of `groups`. A program takes and returns all parts, laid end to end along the dimension named above; an argument that names none is the same for every part. Nothing has to cross between parts.
Inputs may be any that keep to these rules, and one draw needn't show every extreme that they name: `expert_ids`: each row names 2 different experts. One expert, the same on every device, is named by every row. `slot_ids`: among the choices of one aligned block of 4 rows that name one expert, the slot positions are distinct and run from 0 to their count less one.
All inputs are finite; a program needn't handle non-finite values.
Results may differ from a plain program's by a relative error of at most 0.007.
Values may be sent and summed in bfloat16 or wider, within the bound.
A program may use at most 128 MiB of HBM per device.

v0:
```python
import jax
import jax.numpy as jnp
from jax import lax
from jax.sharding import PartitionSpec as P

D = 2048
D_STATE = 16
DT_RANK = 256
EXPERTS = 8
TOPK = 2
CAP = 2
NORM_EPS = 1e-05
STEP_EPS = 1e-06


def expert_ffn(received, gate_proj, up_proj, down_proj):
    gate_val = jnp.einsum("nlcd,ldf->nlcf", received, gate_proj, preferred_element_type=jnp.float32)
    up_val = jnp.einsum("nlcd,ldf->nlcf", received, up_proj, preferred_element_type=jnp.float32)
    hidden = (jax.nn.silu(gate_val) * up_val).astype(jnp.bfloat16)
    return jnp.einsum("nlcf,lfd->nlcd", hidden, down_proj, preferred_element_type=jnp.float32)


def per_device(
    tokens,
    mixer_norm,
    input_proj,
    conv_weight,
    conv_bias,
    conv_state,
    state_proj,
    step_gain,
    step_proj,
    step_bias,
    decay_log,
    skip_gain,
    ssm_state,
    output_proj,
    moe_norm,
    router_weight,
    expert_ids,
    slot_ids,
    gate_proj,
    up_proj,
    down_proj,
):
    head_count = lax.axis_size("head")
    state_index = lax.axis_index("state")
    own_rows = tokens.shape[0]
    tok_f32 = tokens.astype(jnp.float32)
    first_sq = lax.psum(jnp.sum(tok_f32 * tok_f32, axis=1), "state")
    inv_first = lax.rsqrt(first_sq / D + NORM_EPS)[:, None]
    normed = (tok_f32 * inv_first * mixer_norm).astype(jnp.bfloat16)
    branch_part = jnp.einsum(
        "td,kdc->ktc",
        lax.all_gather(normed, "head", axis=0, tiled=True),
        input_proj,
        preferred_element_type=jnp.float32,
    )
    branch_full = lax.psum(branch_part, "state")
    conv_input = branch_full[0]
    gate_branch = branch_full[1]
    window = jnp.concatenate([conv_state, conv_input[None]], axis=0)
    conv_out = jax.nn.silu(jnp.sum(conv_weight[:, None, :] * window, axis=0) + conv_bias)
    new_conv = window[1:]
    proj_part = jnp.dot(
        conv_out.astype(jnp.bfloat16), state_proj, preferred_element_type=jnp.float32
    )
    projected = lax.psum(proj_part, "head")
    step_low = projected[:, :DT_RANK]
    state_slab = decay_log.shape[0]
    b_input = lax.dynamic_slice_in_dim(projected, DT_RANK + state_index * state_slab, state_slab, 1)
    c_output = lax.dynamic_slice_in_dim(
        projected, DT_RANK + D_STATE + state_index * state_slab, state_slab, 1
    )
    step_inv = lax.rsqrt(jnp.mean(step_low * step_low, axis=1, keepdims=True) + STEP_EPS)
    step_normed = (step_low * step_inv * step_gain).astype(jnp.bfloat16)
    step_size = jax.nn.softplus(
        jnp.dot(step_normed, step_proj, preferred_element_type=jnp.float32) + step_bias
    )
    decay_rate = jnp.exp(-step_size[None] * jnp.exp(decay_log)[:, None, :])
    new_state = decay_rate * ssm_state + step_size[None] * b_input.T[:, :, None] * conv_out[None]
    read_part = jnp.sum(c_output.T[:, :, None] * new_state, axis=0)
    readout = lax.psum(read_part, "state")
    mixer_act = ((readout + skip_gain * conv_out) * jax.nn.silu(gate_branch)).astype(jnp.bfloat16)
    mixer_sum = lax.psum_scatter(
        jnp.dot(mixer_act, output_proj, preferred_element_type=jnp.float32),
        "head",
        scatter_dimension=0,
        tiled=True,
    )
    residual = (tok_f32 + mixer_sum).astype(jnp.bfloat16)
    full_rows = lax.all_gather(residual, "state", axis=1, tiled=True).astype(jnp.float32)
    inv_second = lax.rsqrt(jnp.mean(full_rows * full_rows, axis=1, keepdims=True) + NORM_EPS)
    scaled = full_rows * moe_norm
    logits = inv_second * jnp.dot(scaled, router_weight, precision=lax.Precision.HIGHEST)
    row_normed = (scaled * inv_second).astype(jnp.bfloat16)
    expert_hit = expert_ids[:, :, None] == jnp.arange(EXPERTS, dtype=jnp.int32)[None, None, :]
    chosen = jnp.sum(jnp.where(expert_hit, logits[:, None, :], 0.0), axis=2)
    gate_probs = jax.nn.sigmoid(chosen - chosen[:, ::-1])
    kept_mask = slot_ids < CAP
    mix_weight = jnp.where(kept_mask, gate_probs, 0.0)
    slot_hit = slot_ids[:, :, None] == jnp.arange(CAP, dtype=jnp.int32)[None, None, :]
    slot_place = expert_hit[:, :, :, None] & slot_hit[:, :, None, :]
    dispatch = jnp.sum(slot_place.astype(jnp.int32), axis=1).astype(jnp.bfloat16)
    combine_weight = jnp.sum(jnp.where(slot_place, mix_weight[:, :, None, None], 0.0), axis=1)
    outgoing = jnp.einsum(
        "tec,td->ecd", dispatch, row_normed, preferred_element_type=jnp.float32
    ).astype(jnp.bfloat16)
    row_width = outgoing.shape[2]
    local_experts = gate_proj.shape[0]
    expert_groups = EXPERTS // local_experts
    copies = head_count * local_experts // EXPERTS
    outgoing = jnp.broadcast_to(
        outgoing.reshape(expert_groups, 1, local_experts, CAP, row_width),
        (expert_groups, copies, local_experts, CAP, row_width),
    )
    outgoing = outgoing.reshape(head_count, local_experts, CAP, row_width)
    partial_out = expert_ffn(
        lax.all_to_all(outgoing, "head", split_axis=0, concat_axis=0, tiled=True),
        gate_proj,
        up_proj,
        down_proj,
    )
    returned = lax.all_to_all(
        partial_out.astype(jnp.bfloat16), "head", split_axis=0, concat_axis=0, tiled=True
    ).astype(partial_out.dtype)
    per_expert = returned.reshape(expert_groups, copies, local_experts, CAP, row_width).sum(axis=1)
    per_expert = per_expert.reshape(EXPERTS, CAP, row_width)
    expert_mix = jnp.einsum(
        "tec,ecd->td", combine_weight, per_expert, precision=lax.Precision.HIGHEST
    )
    expert_mix = lax.psum_scatter(
        expert_mix.astype(jnp.bfloat16), "state", scatter_dimension=1, tiled=True
    ).astype(jnp.float32)
    layer_out = (residual.astype(jnp.float32) + expert_mix).astype(jnp.bfloat16)
    load_own = jnp.sum(jnp.where(expert_hit & kept_mask[:, :, None], 1.0, 0.0), axis=(0, 1)).astype(
        jnp.float32
    )
    prob_own = jnp.sum(jax.nn.sigmoid(logits), axis=0)
    load_sum, prob_sum = lax.psum((load_own, prob_own), "head")
    total_rows = head_count * own_rows
    aux_value = EXPERTS * jnp.sum(load_sum / (total_rows * TOPK) * (prob_sum / total_rows))
    return (layer_out, new_conv, new_state, load_sum, aux_value.reshape(1))


def solution(mesh):
    return jax.shard_map(
        per_device,
        mesh=mesh,
        in_specs=(
            P(("groups", "head"), "state"),
            P("state"),
            P(None, "state", "head"),
            P(None, "head"),
            P("head"),
            P(None, "groups", "head"),
            P("head", None),
            P(),
            P(None, "head"),
            P("head"),
            P("state", "head"),
            P("head"),
            P("state", "groups", "head"),
            P("head", "state"),
            P(),
            P(),
            P(("groups", "head"), None),
            P(("groups", "head"), None),
            P("head", None, "state"),
            P("head", None, "state"),
            P("head", "state", None),
        ),
        out_specs=(
            P(("groups", "head"), "state"),
            P(None, "groups", "head"),
            P("state", "groups", "head"),
            P("groups"),
            P("groups"),
        ),
        check_vma=False,
    )
```

profile of v0, /device:TPU:0, one launch (start us, length us, event | category | flops | bytes accessed | tf_op | source)
XLA Modules:
  0.0 225.7 jit_solution(13633011839943154887)
XLA Ops:
  8.2 8.4 %psum.42 = f32[4]{0:T(128)S(1)} all-reduce(f32[4]{0:T(128)S(1)} %fusion.46), channel_id=1, replica_groups=mesh['groups'=2,'head'=4,'state'=4] {'state'}, use_global_device_ids=true, to_apply=%region_1.0 | all-reduce | flops 4 | bytes 32 | tf_op jit(solution)/shard_map/psum | solution.py:50
  17.4 13.4 %all-gather = bf16[4,4,512]{2,1,0:T(4,128)(2,1)S(1)} all-gather(bf16[1,4,512]{2,1,0:T(4,128)(2,1)S(1)} %fusion.52), channel_id=1, replica_groups=mesh['groups'=2,'head'=4,'state'=4] {'head'}, dimensions={0}, use_global_device_ids=true | all-gather | bytes 20480 | tf_op jit(solution)/shard_map/all_gather | solution.py:55
  30.8 3.6 %convolution_bitcast_fusion = f32[2,16,2048]{2,1,0:T(8,128)} fusion(bf16[16,512,1]{1,0,2:T(8,128)(2,1)S(1)} %reshape.86, bf16[2,512,2048]{2,1,0:T(8,128)(2,1)} %param.23), kind=kOutput, calls=%fused_computation.6 | convolution fusion | flops 67108864 | bytes 4472832 | tf_op jit(solution)/shard_map/td,kdc->ktc/dot_general | solution.py:53
  37.3 1.2 dynamic-slice
  39.3 27.6 %all-reduce.5.cloned.1.call-done = f32[2,16,2048]{2,1,0:T(8,128)} async-done(((f32[2,16,2048]{2,1,0:T(8,128)}), f32[2,16,2048]{2,1,0:T(8,128)}) %all-reduce.5.cloned.1.call-update) | async-done | bytes 262160 | tf_op jit(solution)/shard_map/psum | solution.py:59
  67.8 1.1 fusion.26
  69.6 1.7 fusion.31
  71.3 19.0 %psum.44 = f32[16,288]{1,0:T(8,128)S(1)} all-reduce(f32[16,288]{1,0:T(8,128)S(1)} %fusion.31), channel_id=1, replica_groups=mesh['groups'=2,'head'=4,'state'=4] {'head'}, use_global_device_ids=true, to_apply=%region_4.5 | all-reduce | flops 4608 | bytes 36864 | tf_op jit(solution)/shard_map/psum | solution.py:68
  90.7 1.5 fusion.56
  92.2 2.7 %multiply_reduce_fusion = (f32[16,2048]{1,0:T(8,128)}, f32[4,16,2048]{2,1,0:T(8,128)}) fusion(f32[4,16]{1,0:T(4,128)S(1)} %copy.53, f32[16,2048]{1,0:T(8,128)S(1)} %divide_multiply_fusion, f32[4,16]{1,0:T(4,128)S(1)} %copy.54, f32[16,2048]{1,0:T(8,128)S(1)} %get-tuple-element.14, f32[4,16,2048]{2,1,0:T(8,128)} %param.33, f32[4,2048]{1,0:T(4,128)S(1)} %exp.33, ...), kind=kLoop, calls=%fused_computation.23 | loop fusion | flops 884736 | bytes 1606144 | tf_op jit(solution)/shard_map/reduce_sum | solution.py:82
  94.9 1.7 fusion.27
  96.6 27.5 %all-reduce.7.cloned.1.call-done = f32[16,2048]{1,0:T(8,128)} async-done(((f32[16,2048]{1,0:T(8,128)}), f32[16,2048]{1,0:T(8,128)}) %all-reduce.7.cloned.1.call-update) | async-done | bytes 131088 | tf_op jit(solution)/shard_map/psum | solution.py:83
  124.1 1.3 fusion.28
  125.5 19.0 %all-reduce = f32[16,512]{1,0:T(8,128)S(1)} all-reduce(f32[16,512]{1,0:T(8,128)S(1)} %fusion.28), channel_id=2, replica_groups=mesh['groups'=2,'head'=4,'state'=4] {'head'}, use_global_device_ids=true, to_apply=%region_8.9.clone | all-reduce | flops 8192 | bytes 65536
  145.2 5.2 %all_gather.7 = bf16[4,2048]{1,0:T(4,128)(2,1)S(1)} all-gather(bf16[4,512]{1,0:T(4,128)(2,1)S(1)} %fusion.49), channel_id=1, replica_groups=mesh['groups'=2,'head'=4,'state'=4] {'state'}, dimensions={1}, use_global_device_ids=true | all-gather | bytes 20480 | tf_op jit(solution)/shard_map/all_gather | solution.py:92
  150.5 1.1 fusion.54
  153.2 3.3 %all-to-all-start = ((bf16[4,2,2,2048]{3,2,1,0:T(2,128)(2,1)}), bf16[4,2,2,2048]{3,2,1,0:T(2,128)(2,1)S(1)}, u32[]{:S(2)}, u32[]{:S(2)}) async-start(bf16[4,2,2,2048]{3,2,1,0:T(2,128)(2,1)} %bitcast.6), calls=%async_computation | async-start | bytes 131072 | tf_op jit(solution)/shard_map/all_to_all | solution.py:119
  156.7 12.1 %all-reduce.1 = (f32[8]{0:T(128)S(1)}, f32[8]{0:T(128)S(1)}) all-reduce(f32[8]{0:T(128)S(1)} %get-tuple-element.5, f32[8]{0:T(128)S(1)} %get-tuple-element.15), channel_id=1, replica_groups=mesh['groups'=2,'head'=4,'state'=4] {'head'}, use_global_device_ids=true, to_apply=%region_15.16 | all-reduce | flops 16 | bytes 128 | tf_op jit(solution)/shard_map/psum | solution.py:140
  168.9 7.5 %fusion.6 = f32[4,2,2,1792]{3,0,2,1:T(4,128)S(1)} fusion(bf16[2,2048,1792]{2,1,0:T(8,128)(2,1)} %param.39, bf16[4,2,2,2048]{3,2,1,0:T(2,128)(2,1)S(1)} %all-to-all-done), kind=kOutput, calls=%fused_computation.7 | convolution fusion | flops 117440512 | bytes 14860288 | tf_op jit(solution)/shard_map/nlcd,ldf->nlcf/dot_general | solution.py:17
  176.4 7.5 %fusion.15 = bf16[4,2,2,1792]{3,0,2,1:T(4,128)(2,1)S(1)} fusion(bf16[2,2048,1792]{2,1,0:T(8,128)(2,1)} %param.40, f32[4,2,2,1792]{3,0,2,1:T(4,128)S(1)} %fusion.6, bf16[4,2,2,2048]{3,2,1,0:T(2,128)(2,1)S(1)} %all-to-all-done), kind=kOutput, calls=%fused_computation.11 | convolution fusion | flops 117612544 | bytes 14917632 | tf_op jit(solution)/shard_map/nlcd,ldf->nlcf/dot_general | solution.py:18
  183.9 2.1 fusion.21
  186.7 3.3 %all-to-all-start.1 = ((bf16[4,2,2,2048]{3,2,1,0:T(2,128)(2,1)}), bf16[4,2,2,2048]{3,2,1,0:T(2,128)(2,1)S(1)}, u32[]{:S(2)}, u32[]{:S(2)}) async-start(bf16[4,2,2,2048]{3,2,1,0:T(2,128)(2,1)} %copy.58), calls=%async_computation.1 | async-start | bytes 131072 | tf_op jit(solution)/shard_map/all_to_all | solution.py:124
  190.1 5.6 %all-to-all-done.1 = bf16[4,2,2,2048]{3,2,1,0:T(2,128)(2,1)S(1)} async-done(((bf16[4,2,2,2048]{3,2,1,0:T(2,128)(2,1)}), bf16[4,2,2,2048]{3,2,1,0:T(2,128)(2,1)S(1)}, u32[]{:S(2)}, u32[]{:S(2)}) %all-to-all-start.1) | async-done | bytes 65568 | tf_op jit(solution)/shard_map/all_to_all | solution.py:124
  198.3 18.1 %reduce-scatter.4.cloned.1.call-done = bf16[512,4]{1,0:T(8,128)(2,1)} async-done(((bf16[2048,4]{1,0:T(8,128)(2,1)}), bf16[512,4]{1,0:T(8,128)(2,1)}) %reduce-scatter.4.cloned.1.call-update) | async-done | bytes 4112
  (55 shorter events, 13.9 us)
Async XLA Ops:
  7.2 117.0 %copy-start = (bf16[2048,512]{1,0:T(8,128)(2,1)S(1)}, bf16[2048,512]{1,0:T(8,128)(2,1)}, u32[]{:S(2)}) copy-start(bf16[2048,512]{1,0:T(8,128)(2,1)} %param.34) | copy-start | bytes 6291460
  7.2 149.4 %copy-start.1 = (s32[4,2]{0,1:T(2,128)S(1)}, s32[4,2]{0,1:T(2,128)}, u32[]{:S(2)}) copy-start(s32[4,2]{0,1:T(2,128)} %param.37) | copy-start | bytes 100
  7.2 149.5 %copy-start.2 = (s32[4,2]{0,1:T(2,128)S(1)}, s32[4,2]{0,1:T(2,128)}, u32[]{:S(2)}) copy-start(s32[4,2]{0,1:T(2,128)} %param.38) | copy-start | bytes 100
  7.2 59.7 %all-reduce.5.cloned.1.call-start = ((), (), s32[]{:S(2)}) async-start(), calls=%async_computation.3 | async-start | bytes 524288 | tf_op jit(solution)/shard_map/psum | solution.py:59
  34.4 89.8 %all-reduce.7.cloned.1.call-start = ((), (), s32[]{:S(2)}) async-start(), calls=%async_computation.4 | async-start | bytes 262144 | tf_op jit(solution)/shard_map/psum | solution.py:83
  153.2 15.7 %all-to-all-start = ((bf16[4,2,2,2048]{3,2,1,0:T(2,128)(2,1)}), bf16[4,2,2,2048]{3,2,1,0:T(2,128)(2,1)S(1)}, u32[]{:S(2)}, u32[]{:S(2)}) async-start(bf16[4,2,2,2048]{3,2,1,0:T(2,128)(2,1)} %bitcast.6), calls=%async_computation | async-start | bytes 131072 | tf_op jit(solution)/shard_map/all_to_all | solution.py:119
  168.9 28.1 %copy-start.3 = (f32[8]{0:T(128)}, f32[8]{0:T(128)S(1)}, u32[]{:S(2)}) copy-start(f32[8]{0:T(128)S(1)} %get-tuple-element.7) | copy-start | bytes 100
  168.9 15.0 %slice-start = ((s8[14680064]{0:T(1024)(128)(4,1)}), s8[4194304]{0:T(1024)(128)(4,1)S(1)}, s32[]{:S(2)}) async-start(s8[14680064]{0:T(1024)(128)(4,1)} %bitcast.71), calls=%async_computation.6 | async-start | bytes 8388608
  168.9 15.0 %slice-start.1 = ((s8[14680064]{0:T(1024)(128)(4,1)}), s8[4194304]{0:T(1024)(128)(4,1)S(1)}, s32[]{:S(2)}) async-start(s8[14680064]{0:T(1024)(128)(4,1)} %bitcast.71), calls=%async_computation.7 | async-start | bytes 8388608
  176.4 7.5 %slice-start.2 = ((s8[14680064]{0:T(1024)(128)(4,1)}), s8[4194304]{0:T(1024)(128)(4,1)S(1)}, s32[]{:S(2)}) async-start(s8[14680064]{0:T(1024)(128)(4,1)} %bitcast.71), calls=%async_computation.8 | async-start | bytes 8388608
  176.4 7.5 %slice-start.3 = ((s8[14680064]{0:T(1024)(128)(4,1)}), s8[2097152]{0:T(1024)(128)(4,1)S(1)}, s32[]{:S(2)}) async-start(s8[14680064]{0:T(1024)(128)(4,1)} %bitcast.71), calls=%async_computation.9 | async-start | bytes 4194304
  186.7 9.0 %all-to-all-start.1 = ((bf16[4,2,2,2048]{3,2,1,0:T(2,128)(2,1)}), bf16[4,2,2,2048]{3,2,1,0:T(2,128)(2,1)S(1)}, u32[]{:S(2)}, u32[]{:S(2)}) async-start(bf16[4,2,2,2048]{3,2,1,0:T(2,128)(2,1)} %copy.58), calls=%async_computation.1 | async-start | bytes 131072 | tf_op jit(solution)/shard_map/all_to_all | solution.py:124
  190.0 26.4 %reduce-scatter.4.cloned.1.call-start = ((), (), s32[]{:S(2)}) async-start(), calls=%async_computation.5 | async-start | bytes 655360
Sparse Core Ops, SparseCore 0:
  34.5 32.3 all-reduce.4
  95.0 29.0 all-reduce.6
  197.2 19.2 reduce-scatter.3
where the time goes:
time: 227 us; the launch traced here: 226 us
  waiting for transfers between devices  78.8 us (35%)
  blocking collectives  77.1 us (34%)
  matrix products  27.5 us (12%)
  between operations  16.4 us (7%)
  other arithmetic  12.6 us (6%)
  local copies, waits for them, and re-layouts  6.69 us (3%)
  starting transfers between devices  6.69 us (3%)
    psum x1, waiting for transfers between devices, per_device(): branch_full = lax.psum(branch_part, 'state')  27.6 us
    psum x1, waiting for transfers between devices, per_device(): readout = lax.psum(read_part, 'state')  27.5 us
    unnamed x1, blocking collectives  19 us
    psum x1, blocking collectives, per_device(): projected = lax.psum(proj_part, 'head')  19 us
    unnamed x4, waiting for transfers between devices  18.2 us
    all_gather x1, blocking collectives, per_device(): lax.all_gather(normed, 'head', axis=0, tiled=True)  13.4 us
    psum x1, blocking collectives, per_device(): load_sum, prob_sum = lax.psum((load_own, prob_own), 'head')  12.1 us
    psum x1, blocking collectives, per_device(): first_sq = lax.psum(jnp.sum(tok_f32 * tok_f32, axis=1), 'state')  8.36 us
  transfers between devices with their start and end apart: 5, of which 4 were waited for; matrix products, arithmetic and copies ran while one was open for 3% of the time, Pallas kernels for 0%

commit v1 on v0

--- a/solution.py
+++ b/solution.py
@@ -56,7 +56,7 @@
         input_proj,
         preferred_element_type=jnp.float32,
     )
-    branch_full = lax.psum(branch_part, "state")
+    branch_full = jnp.sum(lax.all_gather(branch_part, "state"), axis=0)
     conv_input = branch_full[0]
     gate_branch = branch_full[1]
     window = jnp.concatenate([conv_state, conv_input[None]], axis=0)

time: 227 us -> 209 us (0.921)
  waiting for transfers between devices: 78.8 us -> 63.2 us
    psum x1 -> x0, waiting for transfers between devices: 27.6 us -> none  [per_device(): branch_full = lax.psum(branch_part, 'state')]
    all_gather x0 -> x1, waiting for transfers between devices: none -> 12 us  [per_device(): branch_full = jnp.sum(lax.all_gather(branch_part, 'state'), axis=0)]
where the time goes in v1:
time: 209 us; the launch traced here: 208 us
  blocking collectives  77.1 us (37%)
  waiting for transfers between devices  63.2 us (30%)
  matrix products  25.8 us (12%)
  between operations  16.4 us (8%)
  other arithmetic  13.2 us (6%)
  starting transfers between devices  6.69 us (3%)
  local copies, waits for them, and re-layouts  5.8 us (3%)
    psum x1, waiting for transfers between devices, per_device(): readout = lax.psum(read_part, 'state')  27.5 us
    unnamed x1, blocking collectives  19 us
    psum x1, blocking collectives, per_device(): projected = lax.psum(proj_part, 'head')  19 us
    unnamed x4, waiting for transfers between devices  18.2 us
    all_gather x1, blocking collectives, per_device(): lax.all_gather(normed, 'head', axis=0, tiled=True)  13.4 us
    psum x1, blocking collectives, per_device(): load_sum, prob_sum = lax.psum((load_own, prob_own), 'head')  12.1 us
    all_gather x1, waiting for transfers between devices, per_device(): branch_full = jnp.sum(lax.all_gather(branch_part, 'state'), axis=0)  12 us
    psum x1, blocking collectives, per_device(): first_sq = lax.psum(jnp.sum(tok_f32 * tok_f32, axis=1), 'state')  8.36 us
  transfers between devices with their start and end apart: 5, of which 4 were waited for; matrix products, arithmetic and copies ran while one was open for 3% of the time, Pallas kernels for 0%

profile of v1, /device:TPU:0, one launch (start us, length us, event | category | flops | bytes accessed | tf_op | source)
XLA Modules:
  0.0 208.3 jit_solution(6594597893676394273)
XLA Ops:
  8.2 8.4 %psum.35 = f32[4]{0:T(128)S(1)} all-reduce(f32[4]{0:T(128)S(1)} %fusion.46), channel_id=1, replica_groups=mesh['groups'=2,'head'=4,'state'=4] {'state'}, use_global_device_ids=true, to_apply=%region_1.0 | all-reduce | flops 4 | bytes 32 | tf_op jit(solution)/shard_map/psum | solution.py:50
  17.4 13.4 %all-gather.1 = bf16[4,4,512]{2,1,0:T(4,128)(2,1)S(1)} all-gather(bf16[1,4,512]{2,1,0:T(4,128)(2,1)S(1)} %fusion.52), channel_id=1, replica_groups=mesh['groups'=2,'head'=4,'state'=4] {'head'}, dimensions={0}, use_global_device_ids=true | all-gather | bytes 20480 | tf_op jit(solution)/shard_map/all_gather | solution.py:55
  30.8 3.6 %convolution_bitcast_fusion = f32[2,16,2048]{2,1,0:T(8,128)} fusion(bf16[16,512,1]{1,0,2:T(8,128)(2,1)S(1)} %reshape.87, bf16[2,512,2048]{2,1,0:T(8,128)(2,1)} %param.23), kind=kOutput, calls=%fused_computation.6 | convolution fusion | flops 67108864 | bytes 4472832 | tf_op jit(solution)/shard_map/td,kdc->ktc/dot_general | solution.py:53
  35.3 1.2 dynamic-slice
  39.4 12.0 %all-gather.4.cloned.1.call-done = f32[8,16,2048]{2,1,0:T(8,128)} async-done(((f32[2,16,2048]{2,1,0:T(8,128)}), f32[8,16,2048]{2,1,0:T(8,128)}) %all-gather.4.cloned.1.call-update) | async-done | bytes 1048592 | tf_op jit(solution)/shard_map/all_gather | solution.py:59
  51.4 1.3 reduce_sum.113
  52.7 1.1 fusion.26
  54.5 1.7 fusion.31
  56.2 19.0 %psum.36 = f32[16,288]{1,0:T(8,128)S(1)} all-reduce(f32[16,288]{1,0:T(8,128)S(1)} %fusion.31), channel_id=1, replica_groups=mesh['groups'=2,'head'=4,'state'=4] {'head'}, use_global_device_ids=true, to_apply=%region_4.5 | all-reduce | flops 4608 | bytes 36864 | tf_op jit(solution)/shard_map/psum | solution.py:68
  75.5 1.5 fusion.56
  77.1 2.7 %multiply_reduce_fusion = (f32[16,2048]{1,0:T(8,128)}, f32[4,16,2048]{2,1,0:T(8,128)}) fusion(f32[4,16]{1,0:T(4,128)S(1)} %copy.53, f32[16,2048]{1,0:T(8,128)S(1)} %divide_multiply_fusion, f32[4,16]{1,0:T(4,128)S(1)} %copy.54, f32[16,2048]{1,0:T(8,128)S(1)} %get-tuple-element.14, f32[4,16,2048]{2,1,0:T(8,128)} %param.33, f32[4,2048]{1,0:T(4,128)S(1)} %exp.33, ...), kind=kLoop, calls=%fused_computation.23 | loop fusion | flops 884736 | bytes 1606144 | tf_op jit(solution)/shard_map/reduce_sum | solution.py:82
  79.8 1.7 fusion.27
  81.5 27.5 %all-reduce.4.cloned.1.call-done = f32[16,2048]{1,0:T(8,128)} async-done(((f32[16,2048]{1,0:T(8,128)}), f32[16,2048]{1,0:T(8,128)}) %all-reduce.4.cloned.1.call-update) | async-done | bytes 131088 | tf_op jit(solution)/shard_map/psum | solution.py:83
  109.0 1.3 fusion.28
  110.3 19.0 %all-reduce = f32[16,512]{1,0:T(8,128)S(1)} all-reduce(f32[16,512]{1,0:T(8,128)S(1)} %fusion.28), channel_id=3, replica_groups=mesh['groups'=2,'head'=4,'state'=4] {'head'}, use_global_device_ids=true, to_apply=%region_8.9.clone | all-reduce | flops 8192 | bytes 65536
  129.3 5.2 %all_gather.15 = bf16[4,2048]{1,0:T(4,128)(2,1)S(1)} all-gather(bf16[4,512]{1,0:T(4,128)(2,1)S(1)} %fusion.49), channel_id=1, replica_groups=mesh['groups'=2,'head'=4,'state'=4] {'state'}, dimensions={1}, use_global_device_ids=true | all-gather | bytes 20480 | tf_op jit(solution)/shard_map/all_gather | solution.py:92
  135.9 3.3 %all-to-all-start = ((bf16[4,2,2,2048]{3,2,1,0:T(2,128)(2,1)}), bf16[4,2,2,2048]{3,2,1,0:T(2,128)(2,1)S(1)}, u32[]{:S(2)}, u32[]{:S(2)}) async-start(bf16[4,2,2,2048]{3,2,1,0:T(2,128)(2,1)} %bitcast.7), calls=%async_computation | async-start | bytes 131072 | tf_op jit(solution)/shard_map/all_to_all | solution.py:119
  139.4 12.1 %all-reduce.1 = (f32[8]{0:T(128)S(1)}, f32[8]{0:T(128)S(1)}) all-reduce(f32[8]{0:T(128)S(1)} %get-tuple-element.5, f32[8]{0:T(128)S(1)} %get-tuple-element.15), channel_id=1, replica_groups=mesh['groups'=2,'head'=4,'state'=4] {'head'}, use_global_device_ids=true, to_apply=%region_15.16 | all-reduce | flops 16 | bytes 128 | tf_op jit(solution)/shard_map/psum | solution.py:140
  151.5 7.5 %fusion.6 = f32[4,2,2,1792]{3,0,2,1:T(4,128)S(1)} fusion(bf16[2,2048,1792]{2,1,0:T(8,128)(2,1)} %param.39, bf16[4,2,2,2048]{3,2,1,0:T(2,128)(2,1)S(1)} %all-to-all-done), kind=kOutput, calls=%fused_computation.7 | convolution fusion | flops 117440512 | bytes 14860288 | tf_op jit(solution)/shard_map/nlcd,ldf->nlcf/dot_general | solution.py:17
  159.0 7.5 %fusion.15 = bf16[4,2,2,1792]{3,0,2,1:T(4,128)(2,1)S(1)} fusion(bf16[2,2048,1792]{2,1,0:T(8,128)(2,1)} %param.40, f32[4,2,2,1792]{3,0,2,1:T(4,128)S(1)} %fusion.6, bf16[4,2,2,2048]{3,2,1,0:T(2,128)(2,1)S(1)} %all-to-all-done), kind=kOutput, calls=%fused_computation.11 | convolution fusion | flops 117612544 | bytes 14917632 | tf_op jit(solution)/shard_map/nlcd,ldf->nlcf/dot_general | solution.py:18
  166.5 2.1 %fusion.21 = bf16[4,2,2,2048]{3,0,2,1:T(4,128)(2,1)S(1)} fusion(bf16[4,2,2,1792]{3,0,2,1:T(4,128)(2,1)S(1)} %fusion.15, bf16[2,1792,2048]{2,1,0:T(8,128)(2,1)S(1)} %bitcast.73), kind=kOutput, calls=%fused_computation.14 | convolution fusion | flops 117473280 | bytes 14802944 | tf_op jit(solution)/shard_map/nlcf,lfd->nlcd/dot_general | solution.py:20
  169.3 3.3 %all-to-all-start.1 = ((bf16[4,2,2,2048]{3,2,1,0:T(2,128)(2,1)}), bf16[4,2,2,2048]{3,2,1,0:T(2,128)(2,1)S(1)}, u32[]{:S(2)}, u32[]{:S(2)}) async-start(bf16[4,2,2,2048]{3,2,1,0:T(2,128)(2,1)} %copy.58), calls=%async_computation.1 | async-start | bytes 131072 | tf_op jit(solution)/shard_map/all_to_all | solution.py:124
  172.8 5.6 %all-to-all-done.1 = bf16[4,2,2,2048]{3,2,1,0:T(2,128)(2,1)S(1)} async-done(((bf16[4,2,2,2048]{3,2,1,0:T(2,128)(2,1)}), bf16[4,2,2,2048]{3,2,1,0:T(2,128)(2,1)S(1)}, u32[]{:S(2)}, u32[]{:S(2)}) %all-to-all-start.1) | async-done | bytes 65568 | tf_op jit(solution)/shard_map/all_to_all | solution.py:124
  180.9 18.1 %reduce-scatter.4.cloned.1.call-done = bf16[512,4]{1,0:T(8,128)(2,1)} async-done(((bf16[2048,4]{1,0:T(8,128)(2,1)}), bf16[512,4]{1,0:T(8,128)(2,1)}) %reduce-scatter.4.cloned.1.call-update) | async-done | bytes 4112
  (62 shorter events, 11.9 us)
Async XLA Ops:
  7.2 101.8 %copy-start = (bf16[2048,512]{1,0:T(8,128)(2,1)S(1)}, bf16[2048,512]{1,0:T(8,128)(2,1)}, u32[]{:S(2)}) copy-start(bf16[2048,512]{1,0:T(8,128)(2,1)} %param.34) | copy-start | bytes 6291460
  7.2 122.1 %copy-start.1 = (bf16[4,512]{1,0:T(4,128)(2,1)S(1)}, bf16[4,512]{1,0:T(4,128)(2,1)}, u32[]{:S(2)}) copy-start(bf16[4,512]{1,0:T(4,128)(2,1)} %param.21) | copy-start | bytes 12292
  7.2 132.0 %copy-start.3 = (s32[4,2]{0,1:T(2,128)S(1)}, s32[4,2]{0,1:T(2,128)}, u32[]{:S(2)}) copy-start(s32[4,2]{0,1:T(2,128)} %param.37) | copy-start | bytes 100
  7.2 132.1 %copy-start.4 = (s32[4,2]{0,1:T(2,128)S(1)}, s32[4,2]{0,1:T(2,128)}, u32[]{:S(2)}) copy-start(s32[4,2]{0,1:T(2,128)} %param.38) | copy-start | bytes 100
  7.2 127.4 %copy-start.2 = (f32[2048]{0:T(1024)S(1)}, f32[2048]{0:T(1024)}, u32[]{:S(2)}) copy-start(f32[2048]{0:T(1024)} %param.35) | copy-start | bytes 24580
  7.2 127.4 %copy-start.5 = (f32[2048,8]{0,1:T(8,128)S(1)}, f32[2048,8]{0,1:T(8,128)}, u32[]{:S(2)}) copy-start(f32[2048,8]{0,1:T(8,128)} %param.36) | copy-start | bytes 196612
  7.2 44.1 %all-gather.4.cloned.1.call-start = ((), (), s32[]{:S(2)}) async-start(), calls=%async_computation.4 | async-start | bytes 1310720 | tf_op jit(solution)/shard_map/all_gather | solution.py:59
  34.4 74.6 %all-reduce.4.cloned.1.call-start = ((), (), s32[]{:S(2)}) async-start(), calls=%async_computation.3 | async-start | bytes 262144 | tf_op jit(solution)/shard_map/psum | solution.py:83
  135.9 15.7 %all-to-all-start = ((bf16[4,2,2,2048]{3,2,1,0:T(2,128)(2,1)}), bf16[4,2,2,2048]{3,2,1,0:T(2,128)(2,1)S(1)}, u32[]{:S(2)}, u32[]{:S(2)}) async-start(bf16[4,2,2,2048]{3,2,1,0:T(2,128)(2,1)} %bitcast.7), calls=%async_computation | async-start | bytes 131072 | tf_op jit(solution)/shard_map/all_to_all | solution.py:119
  151.5 28.1 %copy-start.6 = (f32[8]{0:T(128)}, f32[8]{0:T(128)S(1)}, u32[]{:S(2)}) copy-start(f32[8]{0:T(128)S(1)} %get-tuple-element.7) | copy-start | bytes 100
  151.5 15.0 %slice-start = ((s8[14680064]{0:T(1024)(128)(4,1)}), s8[4194304]{0:T(1024)(128)(4,1)S(1)}, s32[]{:S(2)}) async-start(s8[14680064]{0:T(1024)(128)(4,1)} %bitcast.72), calls=%async_computation.6 | async-start | bytes 8388608
  151.5 15.0 %slice-start.1 = ((s8[14680064]{0:T(1024)(128)(4,1)}), s8[4194304]{0:T(1024)(128)(4,1)S(1)}, s32[]{:S(2)}) async-start(s8[14680064]{0:T(1024)(128)(4,1)} %bitcast.72), calls=%async_computation.7 | async-start | bytes 8388608
  159.0 7.5 %slice-start.2 = ((s8[14680064]{0:T(1024)(128)(4,1)}), s8[4194304]{0:T(1024)(128)(4,1)S(1)}, s32[]{:S(2)}) async-start(s8[14680064]{0:T(1024)(128)(4,1)} %bitcast.72), calls=%async_computation.8 | async-start | bytes 8388608
  159.0 7.5 %slice-start.3 = ((s8[14680064]{0:T(1024)(128)(4,1)}), s8[2097152]{0:T(1024)(128)(4,1)S(1)}, s32[]{:S(2)}) async-start(s8[14680064]{0:T(1024)(128)(4,1)} %bitcast.72), calls=%async_computation.9 | async-start | bytes 4194304
  169.3 9.0 %all-to-all-start.1 = ((bf16[4,2,2,2048]{3,2,1,0:T(2,128)(2,1)}), bf16[4,2,2,2048]{3,2,1,0:T(2,128)(2,1)S(1)}, u32[]{:S(2)}, u32[]{:S(2)}) async-start(bf16[4,2,2,2048]{3,2,1,0:T(2,128)(2,1)} %copy.58), calls=%async_computation.1 | async-start | bytes 131072 | tf_op jit(solution)/shard_map/all_to_all | solution.py:124
  172.6 26.4 %reduce-scatter.4.cloned.1.call-start = ((), (), s32[]{:S(2)}) async-start(), calls=%async_computation.5 | async-start | bytes 655360
Sparse Core Ops, SparseCore 0:
  34.5 16.7 all-gather.3
  79.9 29.0 all-reduce.3
  179.8 19.2 reduce-scatter.3
